TPU v7x, 32 devices: a whole 2x2x4 slice. The times are simulated.
32 devices in a mesh: grp: 4 (over z), seq: 4 (over y, x), mp: 2 (over core).
Axes of the slice: x: 2, y: 2, z: 4, core: 2. Of those that a mesh axis runs over, the one named last changes fastest.
Arguments:
- queries: bfloat16 [4, 1024, 2048], P('grp', 'seq', 'mp'), may hold values from -400 to 400
- neighbours: bfloat16 [4, 16, 256, 1024], P('grp', 'seq'), may hold values from -6 to 6
- w_key: bfloat16 [1024, 2048], P(('grp', 'seq'), 'mp'), may hold values from -0.1875 to 0.1875
- w_value: bfloat16 [1024, 2048], P(('grp', 'seq'), 'mp'), may hold values from -0.1875 to 0.1875
- lambdas: float32 [16], P('mp'), may hold values from 0.2 to 0.9
- gain: float32 [2048], P('mp'), may hold values from 0.5 to 1.5
- counts: int32 [4], P('grp'), may hold values from 2 to 16, as said below
- d_out: bfloat16 [4, 1024, 2048], P('grp', 'seq', 'mp'), may hold values from -6 to 6
Outputs:
- attended: bfloat16 [4, 1024, 2048], P('grp', 'seq', 'mp')
- d_neigh: float32 [4, 16, 256, 1024], P('grp', 'seq', None, 'mp')
Inputs may be any that keep to these rules, and one draw needn't show every extreme that they name: `counts`: at least one sequence has all 16 groups valid.
All inputs are finite; a program needn't handle non-finite values.
Results may differ from a plain program's by a relative error of at most 0.017.
Values may be sent and summed in bfloat16 or wider, within the bound.
A program may use at most 128 MiB of HBM per device.

v0:
```python
import jax
import jax.numpy as jnp
from jax import lax
from jax.sharding import PartitionSpec as P

epsilon = 1e-06


def from_behind(value, axis, steps):
    count = lax.axis_size(axis)
    initial, last = (max(0, -steps), min(count, count - steps))
    return lax.ppermute(value, axis, [(source, source + steps) for source in range(initial, last)])


def contract_last(left, right):
    return lax.dot_general(
        left, right, (((1,), (1,)), ((), ())), preferred_element_type=jnp.float32
    )


def on_device(queries, neighbours, w_key, w_value, lambdas, gain, counts, d_out):
    group_count = neighbours.shape[1]
    row_count = neighbours.shape[2]
    enc_width = neighbours.shape[3]
    pair_count = lambdas.shape[0]
    group_len = queries.shape[1] // group_count
    key_cols = w_key.shape[1]
    head_dim = key_cols // (2 * pair_count)
    value_dim = w_value.shape[1] // pair_count
    both_cols = key_cols + w_value.shape[1]
    slot_rows = group_count * row_count
    w_both = jnp.concatenate([w_key, w_value], axis=1)
    arriving = from_behind(neighbours[0, group_count - 1], "seq", 1)
    slot_enc = jnp.concatenate([arriving[None], neighbours[0, : group_count - 1]], axis=0)
    flat_rows = slot_enc.reshape(slot_rows, enc_width)
    seq_rows = lax.all_gather(w_both, "seq", axis=0, tiled=True)
    projected = jnp.dot(
        flat_rows,
        lax.all_gather(seq_rows, "grp", axis=0, tiled=True),
        preferred_element_type=jnp.float32,
    )
    projected = projected.reshape(group_count, row_count, both_cols)
    key_heads = projected[..., :key_cols].reshape(group_count, row_count, pair_count, 2, head_dim)
    value_heads = (
        projected[..., key_cols:]
        .astype(jnp.bfloat16)
        .reshape(group_count, row_count, pair_count, value_dim)
    )
    query_heads = queries[0].reshape(group_count, group_len, pair_count, 2, head_dim)
    position = lax.axis_index("seq") * group_count + jnp.arange(group_count, dtype=jnp.int32)
    active = ((position >= 1) & (position < counts[0])).astype(jnp.float32)[:, None, None, None]
    score_scale = head_dim ** (-0.5)
    lambda_b = lambdas[None, :, None, None]
    gain_heads = gain.reshape(pair_count, value_dim)
    scores = (
        jnp.einsum(
            "cqhmd,crhmd->chmqr",
            query_heads.astype(jnp.float32),
            key_heads,
            precision=lax.Precision.HIGHEST,
        )
        * score_scale
    )
    soft_maps = jax.nn.softmax(scores, axis=-1)
    mixed_w = (soft_maps[:, :, 0] - lambda_b * soft_maps[:, :, 1]).astype(jnp.bfloat16)
    heads = jnp.einsum("chqr,crhv->cqhv", mixed_w, value_heads, preferred_element_type=jnp.float32)
    inverse = lax.rsqrt(jnp.mean(heads * heads, axis=-1, keepdims=True) + epsilon)
    normed = heads * inverse
    attended = (normed * gain_heads * active).astype(jnp.bfloat16)
    attended = attended.reshape(1, group_count * group_len, pair_count * value_dim)
    upstream = (
        d_out[0].reshape(group_count, group_len, pair_count, value_dim).astype(jnp.float32) * active
    )
    d_normed = upstream * gain_heads
    d_heads = (
        inverse * (d_normed - normed * jnp.mean(d_normed * normed, axis=-1, keepdims=True))
    ).astype(jnp.bfloat16)
    d_mixed = jnp.einsum(
        "cqhv,crhv->chqr", d_heads, value_heads, preferred_element_type=jnp.float32
    )
    d_values = jnp.einsum(
        "chqr,cqhv->crhv", mixed_w, d_heads, preferred_element_type=jnp.float32
    ).astype(jnp.bfloat16)
    d_probs = jnp.stack([d_mixed, -lambda_b * d_mixed], axis=2)
    d_scores = (
        score_scale * soft_maps * (d_probs - jnp.sum(d_probs * soft_maps, axis=-1, keepdims=True))
    ).astype(jnp.bfloat16)
    d_keys = jnp.einsum(
        "chmqr,cqhmd->crhmd", d_scores, query_heads, preferred_element_type=jnp.float32
    ).astype(jnp.bfloat16)
    d_proj = jnp.concatenate(
        [
            d_keys.reshape(group_count, row_count, key_cols),
            d_values.reshape(group_count, row_count, both_cols - key_cols),
        ],
        axis=-1,
    )
    grad_rows = d_proj.reshape(slot_rows, both_cols)
    seq_rows = lax.all_gather(w_both, "seq", axis=0, tiled=True)
    d_slots = contract_last(grad_rows, lax.all_gather(seq_rows, "grp", axis=0, tiled=True)).reshape(
        group_count, row_count, enc_width
    )
    following = from_behind(d_slots[0], "seq", -1)
    d_own = jnp.concatenate([d_slots[1:], following[None]], axis=0)
    d_share = lax.psum_scatter(d_own, "mp", scatter_dimension=2, tiled=True)
    return (attended, d_share[None])


def solution(mesh):
    in_specs = (
        P("grp", "seq", "mp"),
        P("grp", "seq", None, None),
        P(("grp", "seq"), "mp"),
        P(("grp", "seq"), "mp"),
        P("mp"),
        P("mp"),
        P("grp"),
        P("grp", "seq", "mp"),
    )
    out_specs = (P("grp", "seq", "mp"), P("grp", "seq", None, "mp"))
    return jax.shard_map(
        on_device, mesh=mesh, in_specs=in_specs, out_specs=out_specs, check_vma=False
    )
```

profile of v0, /device:TPU:5, one launch (start us, length us, event | category | flops | bytes accessed | tf_op | source)
XLA Modules:
  0.0 219.1 jit_solution(73672836969083805)
XLA Ops:
  7.2 1.7 pad_maximum_fusion.2
  9.0 28.9 %all-gather.3.cloned.1.call-done = bf16[256,2048]{1,0:T(8,128)(2,1)} async-done(((bf16[64,2048]{1,0:T(8,128)(2,1)}), bf16[256,2048]{1,0:T(8,128)(2,1)}) %all-gather.3.cloned.1.call-update) | async-done | bytes 1048592 | tf_op jit(solution)/shard_map/all_gather | solution.py:36
  38.0 1.9 slice_bitcast_fusion.3
  39.9 2.2 collective-permute-start
  42.1 1.1 convert_bitcast_fusion.2
  43.3 0.7 reshape_squeeze.4
  43.9 1.2 copy.23
  46.0 2.8 %slice_bitcast_fusion.2 = bf16[3,256,1024]{2,1,0:T(8,128)(2,1)} fusion(bf16[1,4,256,1024]{3,2,1,0:T(8,128)(2,1)} %param.9), kind=kLoop, calls=%fused_computation.40 | loop fusion | bytes 3145728 | tf_op jit(solution)/shard_map/squeeze | solution.py:34
  48.8 6.8 %collective-permute-done = bf16[256,1024]{1,0:T(8,128)(2,1)} collective-permute-done((bf16[256,1024]{1,0:T(8,128)(2,1)}, bf16[256,1024]{1,0:T(8,128)(2,1)}, u32[]{:S(2)}, u32[]{:S(2)}) %collective-permute-start) | collective-permute-done | bytes 524320 | tf_op jit(solution)/shard_map/ppermute | solution.py:12
  55.7 64.7 %all-gather.5.cloned.1.call-done = bf16[1024,2048]{1,0:T(8,128)(2,1)} async-done(((bf16[256,2048]{1,0:T(8,128)(2,1)}), bf16[1024,2048]{1,0:T(8,128)(2,1)}) %all-gather.5.cloned.1.call-update) | async-done | bytes 4194320 | tf_op jit(solution)/shard_map/all_gather | solution.py:39
  120.3 6.8 %fusion.7 = f32[4,256,2048]{2,1,0:T(8,128)S(1)} fusion(bf16[1024,2048]{1,0:T(8,128)(2,1)} %all-gather.5.cloned.1.call-done, bf16[3,256,1024]{2,1,0:T(8,128)(2,1)} %slice_bitcast_fusion.2, bf16[1,256,1024]{2,1,0:T(8,128)(2,1)} %bitcast.1), kind=kOutput, calls=%fused_computation.12 | convolution fusion | flops 4296015872 | bytes 14680064 | tf_op jit(solution)/shard_map/dot_general | solution.py:37
  127.2 3.2 %copy-done = f32[4,256,2048]{2,1,0:T(8,128)} copy-done((f32[4,256,2048]{2,1,0:T(8,128)}, f32[4,256,2048]{2,1,0:T(8,128)S(1)}, u32[]{:S(2)}) %copy-start) | copy-done | bytes 8388632
  130.4 2.5 %slice.38 = f32[4,256,1024]{2,1,0:T(8,128)} slice(f32[4,256,2048]{2,1,0:T(8,128)S(1)} %fusion.7), slice={[0:4], [0:256], [0:1024]} | slice | bytes 8388608 | tf_op jit(solution)/shard_map/slice | solution.py:43
  133.0 5.4 %copy.16 = f32[4,256,1024]{1,2,0:T(8,128)} copy(f32[4,256,1024]{2,1,0:T(8,128)} %slice.38) | data formatting | bytes 8388608 | tf_op jit(solution)/shard_map/slice | solution.py:43
  138.3 4.6 %fusion.39 = f32[4,8,2,256,64]{3,4,2,1,0:T(8,128)S(1)} fusion(f32[4,256,8,2,64]{1,4,3,2,0:T(8,128)} %bitcast.93, bf16[4,64,8,2,64]{1,4,3,2,0:T(8,128)(2,1)S(1)} %copy.23), kind=kOutput, calls=%fused_computation.60 | convolution fusion | flops 805306368 | bytes 8912896 | tf_op jit(solution)/shard_map/cqhmd,crhmd->chmqr/dot_general | solution.py:56
  142.9 11.1 %fusion.38 = (f32[4,8,2,64]{3,2,1,0:T(2,128)S(1)}, f32[4,8,2,64,256]{4,3,2,1,0:T(8,128)S(1)}) fusion(f32[4,8,2,256,64]{3,4,2,1,0:T(8,128)S(1)} %fusion.39), kind=kOutput, calls=%fused_computation.59 | output fusion | flops 4194559 | bytes 8404992 | tf_op jit(solution)/shard_map/sub | solution.py:64
  154.1 0.7 broadcast_divide_fusion
  155.3 0.9 slice-done.1
  156.9 0.8 multiply_reduce_fusion.1
  157.7 0.7 multiply_convert_fusion.4
  158.5 0.9 fusion.14
  159.3 0.8 convert_bitcast_fusion
  160.4 1.4 multiply_reduce_fusion
  161.8 1.2 convert_bitcast_fusion.1
  163.0 1.8 copy.24
  165.3 1.6 copy.27
  167.5 4.6 %fusion.1 = f32[1024,1024]{1,0:T(8,128)S(1)} fusion(bf16[1024,2048]{1,0:T(8,128)(2,1)S(1)} %copy-done.4, bf16[1024,1024]{0,1:T(8,128)(2,1)S(1)} %bitcast.100, bf16[1024,1024]{0,1:T(8,128)(2,1)S(1)} %bitcast.99), kind=kOutput, calls=%fused_computation.3 | convolution fusion | flops 4303355904 | bytes 12582912 | tf_op jit(solution)/shard_map/dot_general | solution.py:16
  172.1 3.1 %collective-permute-start.1 = (f32[256,1024]{1,0:T(8,128)S(1)}, f32[256,1024]{1,0:T(8,128)S(1)}, u32[]{:S(2)}, u32[]{:S(2)}) collective-permute-start(f32[256,1024]{1,0:T(8,128)S(1)} %slice.43), channel_id=1, source_target_pairs={{2,0},{4,2},{6,4},{3,1},{5,3},{7,5},{10,8},{12,10},{14,12},{11,9},... | collective-permute-start | bytes 3145736 | tf_op jit(solution)/shard_map/ppermute | solution.py:12
  175.6 22.3 %collective-permute-done.1 = f32[256,1024]{1,0:T(8,128)S(1)} collective-permute-done((f32[256,1024]{1,0:T(8,128)S(1)}, f32[256,1024]{1,0:T(8,128)S(1)}, u32[]{:S(2)}, u32[]{:S(2)}) %collective-permute-start.1) | collective-permute-done | bytes 1048608 | tf_op jit(solution)/shard_map/ppermute | solution.py:12
  197.9 2.2 %pad_maximum_fusion.1 = f32[4,256,1024]{2,1,0:T(8,128)} fusion(f32[1,256,1024]{2,1,0:T(8,128)S(1)} %bitcast.101, f32[3,256,1024]{2,1,0:T(8,128)S(1)} %bitcast.94), kind=kLoop, calls=%fused_computation.7 | loop fusion | flops 1048576 | bytes 8388608 | tf_op jit(solution)/shard_map/concatenate | solution.py:104
  200.5 1.0 reshape.59
  201.5 11.1 %reduce-scatter.2.cloned.1.call-done = f32[4,256,512]{2,1,0:T(8,128)} async-done(((f32[4,256,1024]{2,1,0:T(8,128)}), f32[4,256,512]{2,1,0:T(8,128)}) %reduce-scatter.2.cloned.1.call-update) | async-done | bytes 2097168 | tf_op jit(solution)/shard_map/reduce_scatter | solution.py:105
  (32 shorter events, 3.7 us)
Async XLA Ops:
  7.2 36.1 %copy-start.1 = (bf16[1,256,1024]{2,1,0:T(8,128)(2,1)S(1)}, bf16[1,256,1024]{2,1,0:T(8,128)(2,1)}, u32[]{:S(2)}) copy-start(bf16[1,256,1024]{2,1,0:T(8,128)(2,1)} %param.8) | copy-start | bytes 1572868
  7.2 30.8 %all-gather.3.cloned.1.call-start = ((), (), s32[]{:S(2)}) async-start(), calls=%async_computation.1 | async-start | bytes 1310720 | tf_op jit(solution)/shard_map/all_gather | solution.py:36
  9.0 111.4 %all-gather.5.cloned.1.call-start = ((), (), s32[]{:S(2)}) async-start(), calls=%async_computation.2 | async-start | bytes 5242880 | tf_op jit(solution)/shard_map/all_gather | solution.py:39
  38.0 8.0 %copy-start.3 = (f32[8]{0:T(128)S(1)}, f32[8]{0:T(128)}, u32[]{:S(2)}) copy-start(f32[8]{0:T(128)} %param.12) | copy-start | bytes 100
  38.0 174.6 %reduce-scatter.2.cloned.1.call-start = ((), (), s32[]{:S(2)}) async-start(), calls=%async_computation.3 | async-start | bytes 6291456 | tf_op jit(solution)/shard_map/reduce_scatter | solution.py:105
  39.9 15.7 %collective-permute-start = (bf16[256,1024]{1,0:T(8,128)(2,1)}, bf16[256,1024]{1,0:T(8,128)(2,1)}, u32[]{:S(2)}, u32[]{:S(2)}) collective-permute-start(bf16[256,1024]{1,0:T(8,128)(2,1)} %slice_bitcast_fusion.3), channel_id=1, source_target_pairs={{0,2},{2,4},{4,6},{1,3},{3,5},{5,7},{8,10},{10,12},{12,14},{9,11},... | collective-permute-start | bytes 1572872 | tf_op jit(solution)/shard_map/ppermute | solution.py:12
  127.2 3.2 %copy-start = (f32[4,256,2048]{2,1,0:T(8,128)}, f32[4,256,2048]{2,1,0:T(8,128)S(1)}, u32[]{:S(2)}) copy-start(f32[4,256,2048]{2,1,0:T(8,128)S(1)} %fusion.7) | copy-start | bytes 25165828
  142.9 12.4 %slice-start = ((s8[8388608]{0:T(1024)(128)(4,1)}), s8[4194304]{0:T(1024)(128)(4,1)S(1)}, s32[]{:S(2)}) async-start(s8[8388608]{0:T(1024)(128)(4,1)} %bitcast.91), calls=%async_computation.4 | async-start | bytes 8388608
  154.1 2.2 slice-start.1
  156.2 0.7 copy-start.2
  165.3 2.2 %copy-start.4 = (bf16[1024,2048]{1,0:T(8,128)(2,1)S(1)}, bf16[1024,2048]{1,0:T(8,128)(2,1)}, u32[]{:S(2)}) copy-start(bf16[1024,2048]{1,0:T(8,128)(2,1)} %all-gather.5.cloned.1.call-done) | copy-start | bytes 12582916
  172.1 25.8 %collective-permute-start.1 = (f32[256,1024]{1,0:T(8,128)S(1)}, f32[256,1024]{1,0:T(8,128)S(1)}, u32[]{:S(2)}, u32[]{:S(2)}) collective-permute-start(f32[256,1024]{1,0:T(8,128)S(1)} %slice.43), channel_id=1, source_target_pairs={{2,0},{4,2},{6,4},{3,1},{5,3},{7,5},{10,8},{12,10},{14,12},{11,9},... | collective-permute-start | bytes 3145736 | tf_op jit(solution)/shard_map/ppermute | solution.py:12
Sparse Core Ops, SparseCore 0:
  10.4 27.5 all-gather.2
  39.5 80.7 all-gather.4
  200.3 12.2 reduce-scatter.1
where the time goes:
time: 220 us; the launch traced here: 219 us
  waiting for transfers between devices  134 us (61%)
  local copies, waits for them, and re-layouts  25.1 us (11%)
  other arithmetic  20.7 us (9%)
  matrix products  19.4 us (9%)
  between operations  14.7 us (7%)
  starting transfers between devices  5.38 us (2%)
    all_gather x1, waiting for transfers between devices, on_device(): lax.all_gather(seq_rows, 'grp', axis=0, tiled=True)  64.7 us
    ppermute x2, waiting for transfers between devices, from_behind(): lax.ppermute(value, axis, [(source, source + steps) for source in range(i...  29.1 us
    all_gather x1, waiting for transfers between devices, on_device(): seq_rows = lax.all_gather(w_both, 'seq', axis=0, tiled=True)  28.9 us
    sub x1, other arithmetic, on_device(): soft_maps = jax.nn.softmax(scores, axis=-1)  11.1 us
    reduce_scatter x1, waiting for transfers between devices, on_device(): d_share = lax.psum_scatter(d_own, 'mp', scatter_dimension=2, tiled=True)  11.1 us
    slice x2, local copies, waits for them, and re-layouts, on_device(): projected[..., :key_cols]  7.9 us
    dot_general x1, matrix products, on_device(): jnp.dot(flat_rows, lax.all_gather(seq_rows, 'grp', axis=0, tiled=True), p...  6.85 us
    unnamed x17, local copies, waits for them, and re-layouts  5.45 us
  transfers between devices with their start and end apart: 5, of which 5 were waited for; matrix products, arithmetic and copies ran while one was open for 4% of the time, Pallas kernels for 0%

commit v1 on v0

v1 whole, which is shorter than its diff:
```python
import functools

import jax
import jax.numpy as jnp
from jax import lax
from jax.experimental import pallas as pl
from jax.experimental.pallas import tpu as pltpu
from jax.sharding import PartitionSpec as P

EPSILON = 1e-06
MESH = pl.DeviceIdType.MESH
NT = (((1,), (1,)), ((), ()))
TN = (((0,), (0,)), ((), ()))


def dot(left, right, dims=(((1,), (0,)), ((), ()))):
    return lax.dot_general(left, right, dims, preferred_element_type=jnp.float32)


def kernel(
    sizes,
    lambdas,
    counts,
    q_hbm,
    n_hbm,
    wk_hbm,
    wv_hbm,
    gain,
    do_hbm,
    att,
    d_out,
    x,
    q,
    do,
    wk,
    wv,
    acc,
    send,
    got,
    edge,
    local_sem,
    own_sem,
    x_send,
    x_recv,
    p1_send,
    p1_recv,
    p2_send,
    p2_recv,
    g_send,
    g_recv,
    e_send,
    e_recv,
):
    n_grp, n_seq, n_mp, w_seq, chunks, pairs = sizes
    groups, rows, enc = x.shape
    group_len = q.shape[0] // groups
    cols = wk.shape[-1]
    pair_cols = cols // pairs
    head_dim = pair_cols // 2
    half = enc // n_mp
    grp, seq, mp = lax.axis_index("grp"), lax.axis_index("seq"), lax.axis_index("mp")
    w_pos = seq if w_seq > 1 else 0
    following = lax.rem(seq + 1, n_seq)
    preceding = lax.rem(seq + n_seq - 1, n_seq)

    own = []
    for c in range(chunks):
        for kind, (src, dst) in enumerate(((wk_hbm, wk), (wv_hbm, wv))):
            own.append(
                pltpu.make_async_copy(
                    src.at[:, pl.ds(c * cols, cols)], dst.at[c, grp, w_pos], own_sem.at[c, kind]
                )
            )
    for copy in own:
        copy.start()
    local = [
        pltpu.make_async_copy(n_hbm.at[pl.ds(0, groups - 1)], x.at[pl.ds(1, groups - 1)], local_sem.at[0]),
        pltpu.make_async_copy(q_hbm, q, local_sem.at[1]),
        pltpu.make_async_copy(do_hbm, do, local_sem.at[2]),
    ]
    for copy in local:
        copy.start()

    others = [{"grp": lax.rem(grp + o, n_grp)} for o in range(1, n_grp)]
    others += [{"seq": lax.rem(seq + o, n_seq)} for o in (range(1, n_seq) if w_seq > 1 else (1, n_seq - 1))]
    for o in range(1, n_mp):
        partner = lax.rem(mp + o, n_mp)
        others += [{"mp": partner}, {"seq": following, "mp": partner}, {"seq": preceding, "mp": partner}]
    barrier = pltpu.get_barrier_semaphore()
    for device in others:
        pl.semaphore_signal(barrier, inc=1, device_id=device, device_id_type=MESH)
    pl.semaphore_wait(barrier, len(others))

    def remote(src, dst, send_sem, recv_sem, device):
        return pltpu.make_async_remote_copy(
            src_ref=src, dst_ref=dst, send_sem=send_sem, recv_sem=recv_sem, device_id=device, device_id_type=MESH
        )

    def over_grp(ref, sems, c, kind, block):
        return [
            remote(block, block, sems[0].at[c, kind, o], sems[1].at[c, kind, o], {"grp": lax.rem(grp + o, n_grp)})
            for o in range(1, n_grp)
        ]

    def over_seq(ref, sems, c, kind, block):
        return [
            remote(block, block, sems[0].at[c, kind, o], sems[1].at[c, kind, o], {"seq": lax.rem(seq + o, n_seq)})
            for o in range(1, w_seq)
        ]

    one, two = (p1_send, p1_recv), (p2_send, p2_recv)
    first = [
        over_seq(wk, one, c, 0, wk.at[c, grp, w_pos]) + over_grp(wv, one, c, 1, wv.at[c, grp, w_pos])
        for c in range(chunks)
    ]
    second = [
        over_grp(wk, two, c, 0, wk.at[c, grp]) + over_seq(wv, two, c, 1, wv.at[c, :, w_pos]) for c in range(chunks)
    ]
    edge_in = remote(n_hbm.at[groups - 1], x.at[0], x_send, x_recv, {"seq": following})

    def start_first(c):
        own[2 * c].wait()
        own[2 * c + 1].wait()
        for copy in first[c]:
            copy.start()

    def start_second(c):
        for copy in first[c]:
            copy.wait_recv()
        for copy in second[c]:
            copy.start()

    start_first(0)
    edge_in.start()
    for c in range(1, chunks):
        start_first(c)
        start_second(c - 1)
    start_second(chunks - 1)

    for copy in local:
        copy.wait()
    edge_in.wait_recv()

    scale = head_dim ** (-0.5)
    lane = lax.broadcasted_iota(jnp.int32, (group_len, pair_cols), 1)
    on_first = lane < head_dim

    def slot_step(c, u):
        w_k = wk[c].reshape(enc, cols)
        w_v = wv[c].reshape(enc, cols)
        enc_rows = x[u]
        keys = dot(enc_rows, w_k)
        vals = dot(enc_rows, w_v).astype(jnp.bfloat16)
        position = seq * groups + u
        active = (jnp.clip(position, 0, 1) * jnp.clip(counts[0] - position, 0, 1)).astype(jnp.float32)
        tokens = pl.ds(pl.multiple_of(u * group_len, group_len), group_len)
        d_keys, d_vals = [], []
        for p in range(pairs):
            at = pl.ds((c * pairs + p) * pair_cols, pair_cols)
            here = slice(p * pair_cols, (p + 1) * pair_cols)
            lam = lambdas[c * pairs + p]
            query = q[tokens, at]
            zero = jnp.zeros_like(query)
            q2 = jnp.concatenate([jnp.where(on_first, query, zero), jnp.where(on_first, zero, query)], axis=0)
            key = keys[:, here]
            value = vals[:, here]
            key_hi = key.astype(jnp.bfloat16)
            key_lo = (key - key_hi.astype(jnp.float32)).astype(jnp.bfloat16)
            scores = (
                dot(jnp.concatenate([q2, q2], axis=1), jnp.concatenate([key_hi, key_lo], axis=1), NT) * scale
            )
            top = jnp.max(scores, axis=-1, keepdims=True)
            e = jnp.exp(scores - top)
            probs = e * (1.0 / jnp.sum(e, axis=-1, keepdims=True))
            mix = (probs[:group_len] - lam * probs[group_len:]).astype(jnp.bfloat16)
            heads = dot(mix, value)
            inverse = lax.rsqrt(jnp.mean(heads * heads, axis=-1, keepdims=True) + EPSILON)
            normed = heads * inverse
            g = gain[:, at]
            att[tokens, at] = (normed * g * active).astype(jnp.bfloat16)
            dn = do[tokens, at].astype(jnp.float32) * active * g
            d_heads = (inverse * (dn - normed * jnp.mean(dn * normed, axis=-1, keepdims=True))).astype(jnp.bfloat16)
            d_mix = dot(d_heads, value, NT)
            d_vals.append(dot(mix, d_heads, TN).astype(jnp.bfloat16))
            d_probs = jnp.concatenate([d_mix, -lam * d_mix], axis=0)
            total = jnp.sum(d_probs * probs, axis=-1, keepdims=True)
            d_scores = (scale * probs * (d_probs - total)).astype(jnp.bfloat16)
            d_keys.append(dot(d_scores, q2, TN).astype(jnp.bfloat16))
        grad = dot(jnp.concatenate(d_keys, axis=1), w_k, NT) + dot(jnp.concatenate(d_vals, axis=1), w_v, NT)
        if c == 0:
            acc[u] = grad
        else:
            acc[u] += grad

    def arrived(c):
        for copy in second[c]:
            copy.wait_recv()

    for c in range(chunks - 1):
        arrived(c)

        def step(u, carry, c=c):
            slot_step(c, u)
            return carry

        lax.fori_loop(0, groups, step, 0)

    last = chunks - 1
    arrived(last)
    mine = pl.ds(pl.multiple_of(mp * half, half), half)

    slot_step(last, 0)
    edge_out = []
    for o in range(n_mp):
        core = lax.rem(mp + o, n_mp)
        send[0, o] = acc[0, :, pl.ds(pl.multiple_of(core * half, half), half)].astype(jnp.bfloat16)
        edge_out.append(
            remote(send.at[0, o], edge.at[o], e_send.at[o], e_recv.at[o], {"seq": preceding, "mp": core})
        )
    for copy in edge_out:
        copy.start()

    def exchange(u, o):
        return remote(
            send.at[u, o], got.at[u, o], g_send.at[u, o], g_recv.at[u, o], {"mp": lax.rem(mp + o, n_mp)}
        )

    def last_step(u, carry):
        slot_step(last, u)
        for o in range(1, n_mp):
            core = lax.rem(mp + o, n_mp)
            send[u, o] = acc[u, :, pl.ds(pl.multiple_of(core * half, half), half)].astype(jnp.bfloat16)
            exchange(u, o).start()
        return carry

    lax.fori_loop(1, groups, last_step, 0)

    for copy in edge_out:
        copy.wait()
    total = edge[0].astype(jnp.float32)
    for o in range(1, n_mp):
        total += edge[o].astype(jnp.float32)
    d_out[groups - 1] = total

    def finish(u, carry):
        total = acc[u, :, mine]
        for o in range(1, n_mp):
            exchange(u, o).wait()
            total += got[u, o].astype(jnp.float32)
        d_out[u - 1] = total
        return carry

    lax.fori_loop(1, groups, finish, 0)
    for c in range(chunks):
        for copy in first[c] + second[c]:
            copy.wait_send()
    edge_in.wait_send()


def on_device(mesh_shape, queries, neighbours, w_key, w_value, lambdas, gain, counts, d_out):
    n_grp, n_seq, n_mp = (mesh_shape[name] for name in ("grp", "seq", "mp"))
    groups, rows, enc = neighbours.shape[1:]
    tokens, width = queries.shape[1:]
    w_seq = n_seq
    if w_key.shape[0] % 16:
        w_key = lax.all_gather(w_key, "seq", axis=0, tiled=True)
        w_value = lax.all_gather(w_value, "seq", axis=0, tiled=True)
        w_seq = 1
    w_rows = w_key.shape[0]
    pair_count = lambdas.shape[0]
    pairs = 2 if pair_count % 2 == 0 else 1
    chunks = pair_count // pairs
    cols = w_key.shape[1] // chunks
    half = enc // n_mp
    bf16, f32 = jnp.bfloat16, jnp.float32
    vmem = pl.BlockSpec(memory_space=pltpu.VMEM)
    smem = pl.BlockSpec(memory_space=pltpu.SMEM)
    hbm = pl.BlockSpec(memory_space=pl.ANY)
    dma = pltpu.SemaphoreType.DMA
    att, d_neigh = pl.pallas_call(
        functools.partial(kernel, (n_grp, n_seq, n_mp, w_seq, chunks, pairs)),
        out_shape=(
            jax.ShapeDtypeStruct((tokens, width), bf16),
            jax.ShapeDtypeStruct((groups, rows, half), f32),
        ),
        in_specs=[smem, smem, hbm, hbm, hbm, hbm, vmem, hbm],
        out_specs=(vmem, vmem),
        scratch_shapes=[
            pltpu.VMEM((groups, rows, enc), bf16),
            pltpu.VMEM((tokens, width), bf16),
            pltpu.VMEM((tokens, width), bf16),
            pltpu.VMEM((chunks, n_grp, w_seq, w_rows, cols), bf16),
            pltpu.VMEM((chunks, n_grp, w_seq, w_rows, cols), bf16),
            pltpu.VMEM((groups, rows, enc), f32),
            pltpu.VMEM((groups, n_mp, rows, half), bf16),
            pltpu.VMEM((groups, n_mp, rows, half), bf16),
            pltpu.VMEM((n_mp, rows, half), bf16),
            dma((3,)),
            dma((chunks, 2)),
            dma,
            dma,
            dma((chunks, 2, max(n_grp, w_seq))),
            dma((chunks, 2, max(n_grp, w_seq))),
            dma((chunks, 2, max(n_grp, w_seq))),
            dma((chunks, 2, max(n_grp, w_seq))),
            dma((groups, n_mp)),
            dma((groups, n_mp)),
            dma((n_mp,)),
            dma((n_mp,)),
        ],
        compiler_params=pltpu.CompilerParams(
            collective_id=0, has_side_effects=True, vmem_limit_bytes=60 * 1024 * 1024
        ),
    )(lambdas, counts, queries[0], neighbours[0], w_key, w_value, gain.reshape(1, -1), d_out[0])
    return att[None], d_neigh[None]


def solution(mesh):
    in_specs = (
        P("grp", "seq", "mp"),
        P("grp", "seq", None, None),
        P(("grp", "seq"), "mp"),
        P(("grp", "seq"), "mp"),
        P("mp"),
        P("mp"),
        P("grp"),
        P("grp", "seq", "mp"),
    )
    out_specs = (P("grp", "seq", "mp"), P("grp", "seq", None, "mp"))
    return jax.shard_map(
        functools.partial(on_device, dict(mesh.shape)),
        mesh=mesh,
        in_specs=in_specs,
        out_specs=out_specs,
        check_vma=False,
    )
```

time: 220 us -> 108 us (0.49)
  waiting for transfers between devices: 134 us -> 0 us
  Pallas kernels: 0 us -> 101 us
  other arithmetic: 20.7 us -> 0 us
  local copies, waits for them, and re-layouts: 25.1 us -> 4.95 us
  matrix products: 19.4 us -> 0 us
  between operations: 14.7 us -> 1.29 us
  starting transfers between devices: 5.38 us -> 0 us
    pallas_call x0 -> x1, Pallas kernels: none -> 101 us  [on_device(): pl.pallas_call(functools.partial(kernel, (n_grp, n_seq, n_mp, w_seq, chun...]
    all_gather x2 -> x0, waiting for transfers between devices: 93.6 us -> none  [the longest x1 64.7 us: on_device(): lax.all_gather(seq_rows, 'grp', axis=0, tiled=True)]
    ppermute x2 -> x0, waiting for transfers between devices: 29.1 us -> none  [from_behind(): lax.ppermute(value, axis, [(source, source + steps) for source in range(i...]
    dot_general x7 -> x0, matrix products: 19.4 us -> none  [the longest x1 6.85 us: on_device(): jnp.dot(flat_rows, lax.all_gather(seq_rows, 'grp', axis=0, tiled=True), p...]
    sub x1 -> x0, other arithmetic: 11.1 us -> none  [on_device(): soft_maps = jax.nn.softmax(scores, axis=-1)]
    reduce_scatter x1 -> x0, waiting for transfers between devices: 11.1 us -> none  [on_device(): d_share = lax.psum_scatter(d_own, 'mp', scatter_dimension=2, tiled=True)]
    slice x4 -> x0, local copies, waits for them, and re-layouts: 8.34 us -> none  [the longest x2 7.9 us: on_device(): projected[..., :key_cols]]
    ppermute x2 -> x0, starting transfers between devices: 5.26 us -> none  [from_behind(): lax.ppermute(value, axis, [(source, source + steps) for source in range(i...]
  transfers between devices with their start and end apart: 5 -> 0, of which waited for: 5 -> 0; matrix products, arithmetic and copies ran while one was open for 4% -> 0% of each run, Pallas kernels for 0% -> 0%
where the time goes in v1:
time: 108 us
  Pallas kernels  101 us (94%)
  local copies, waits for them, and re-layouts  4.95 us (5%)
  between operations  1.29 us (1%)
    pallas_call x1, Pallas kernels, on_device(): pl.pallas_call(functools.partial(kernel, (n_grp, n_seq, n_mp, w_seq, chun...  101 us
    unnamed x2, local copies, waits for them, and re-layouts  4.95 us

profile of v1, /device:TPU:5, one launch (start us, length us, event | category | flops | bytes accessed | tf_op | source)
XLA Modules:
  0.0 107.6 jit_solution(12353453453145499485)
XLA Ops:
  1.3 101.4 %shard_map.95 = (bf16[256,1024]{1,0:T(8,128)(2,1)}, f32[4,256,512]{2,1,0:T(8,128)}) custom-call(f32[8]{0:T(128)} %lambdas.1, s32[1]{0:T(128)S(6)} %copy.12.counts, bf16[256,1024]{1,0:T(8,128)(2,1)} %bitcast.8, bf16[4,256,1024]{2,1,0:T(8,128)(2,1)} %bitcast.6, bf16[64,1024]{1,0:T(8,128)(2,1)} %wk_hbm.1, bf16[64,1024]{1,0:T(8,128)(2,1)} %wv_hbm.1, ...), custom_call_target="tpu_custom_call" | custom-call | tf_op jit(solution)/shard_map/pallas_call | solution.py:280
  102.7 1.9 %copy.13 = bf16[1,256,1024]{2,1,0:T(8,128)(2,1)} copy(bf16[1,256,1024]{2,1,0:T(8,128)(2,1)} %bitcast.10) | data formatting | bytes 1048576
  104.6 3.1 %copy.14 = f32[1,4,256,512]{3,2,1,0:T(8,128)} copy(f32[1,4,256,512]{3,2,1,0:T(8,128)} %bitcast.7) | data formatting | bytes 4194304

commit v2 on v1

--- a/solution.py
+++ b/solution.py
@@ -96,50 +96,93 @@
             src_ref=src, dst_ref=dst, send_sem=send_sem, recv_sem=recv_sem, device_id=device, device_id_type=MESH
         )
 
-    def over_grp(ref, sems, c, kind, block):
+    def over_grp(sems, c, kind, block):
         return [
             remote(block, block, sems[0].at[c, kind, o], sems[1].at[c, kind, o], {"grp": lax.rem(grp + o, n_grp)})
             for o in range(1, n_grp)
         ]
 
-    def over_seq(ref, sems, c, kind, block):
+    def over_seq(sems, c, kind, block):
         return [
             remote(block, block, sems[0].at[c, kind, o], sems[1].at[c, kind, o], {"seq": lax.rem(seq + o, n_seq)})
             for o in range(1, w_seq)
         ]
 
-    one, two = (p1_send, p1_recv), (p2_send, p2_recv)
-    first = [
-        over_seq(wk, one, c, 0, wk.at[c, grp, w_pos]) + over_grp(wv, one, c, 1, wv.at[c, grp, w_pos])
-        for c in range(chunks)
+    first, second, onward = [], [], []
+    for c in range(chunks):
+        early, late, relay = [], [], []
+        for kind, ref in enumerate((wk, wv)):
+            early += over_grp((p1_send, p1_recv), c, kind, ref.at[c, grp, w_pos])
+            block = ref.at[c, :, w_pos]
+            if w_seq == 4:
+                right = lax.rem(seq, 2) * 2 + 1 - seq // 2
+                left = (1 - lax.rem(seq, 2)) * 2 + seq // 2
+                for o, device in ((1, right), (2, left)):
+                    late.append(
+                        remote(block, block, p2_send.at[c, kind, o], p2_recv.at[c, kind, o], {"seq": device})
+                    )
+                source, target = (left, right) if kind == 0 else (right, left)
+                passed = ref.at[c, :, source]
+                relay.append(
+                    (
+                        late[2 * kind + kind],
+                        remote(passed, passed, p2_send.at[c, kind, 3], p2_recv.at[c, kind, 3], {"seq": target}),
+                    )
+                )
+            else:
+                late += over_seq((p2_send, p2_recv), c, kind, block)
+        first.append(early)
+        second.append(late)
+        onward.append(relay)
+    part = pl.ds(pl.multiple_of(mp * (rows // n_mp), rows // n_mp), rows // n_mp)
+    edge_in = remote(n_hbm.at[groups - 1, part], x.at[0, part], x_send.at[0], x_recv.at[0], {"seq": following})
+    edge_on = [
+        remote(x.at[0, part], x.at[0, part], x_send.at[o], x_recv.at[o], {"mp": lax.rem(mp + o, n_mp)})
+        for o in range(1, n_mp)
     ]
-    second = [
-        over_grp(wk, two, c, 0, wk.at[c, grp]) + over_seq(wv, two, c, 1, wv.at[c, :, w_pos]) for c in range(chunks)
-    ]
-    edge_in = remote(n_hbm.at[groups - 1], x.at[0], x_send, x_recv, {"seq": following})
 
     def start_first(c):
-        own[2 * c].wait()
-        own[2 * c + 1].wait()
-        for copy in first[c]:
-            copy.start()
+        if c < chunks:
+            own[2 * c].wait()
+            own[2 * c + 1].wait()
+            for copy in first[c]:
+                copy.start()
 
     def start_second(c):
-        for copy in first[c]:
-            copy.wait_recv()
-        for copy in second[c]:
-            copy.start()
+        if c < chunks:
+            for copy in first[c]:
+                copy.wait_recv()
+            for copy in second[c]:
+                copy.start()
+            start_first(c + 2)
+
+    def start_onward(c):
+        if c < chunks:
+            for arrival, copy in onward[c]:
+                arrival.wait_recv()
+                copy.start()
+
+    def arrived(c):
+        passed_on = [arrival for arrival, _ in onward[c]]
+        for copy in second[c] + [copy for _, copy in onward[c]]:
+            if not any(copy is other for other in passed_on):
+                copy.wait_recv()
+        start_second(c + 2)
+        start_onward(c + 1)
 
     start_first(0)
     edge_in.start()
-    for c in range(1, chunks):
-        start_first(c)
-        start_second(c - 1)
-    start_second(chunks - 1)
-
+    start_first(1)
+    start_second(0)
+    edge_in.wait_recv()
+    for copy in edge_on:
+        copy.start()
+    start_second(1)
+    start_onward(0)
     for copy in local:
         copy.wait()
-    edge_in.wait_recv()
+    for copy in edge_on:
+        copy.wait_recv()
 
     scale = head_dim ** (-0.5)
     lane = lax.broadcasted_iota(jnp.int32, (group_len, pair_cols), 1)
@@ -192,10 +235,6 @@
         else:
             acc[u] += grad
 
-    def arrived(c):
-        for copy in second[c]:
-            copy.wait_recv()
-
     for c in range(chunks - 1):
         arrived(c)
 
@@ -252,9 +291,11 @@
 
     lax.fori_loop(1, groups, finish, 0)
     for c in range(chunks):
-        for copy in first[c] + second[c]:
+        for copy in first[c] + second[c] + [copy for _, copy in onward[c]]:
             copy.wait_send()
     edge_in.wait_send()
+    for copy in edge_on:
+        copy.wait_send()
 
 
 def on_device(mesh_shape, queries, neighbours, w_key, w_value, lambdas, gain, counts, d_out):
@@ -297,8 +338,8 @@
             pltpu.VMEM((n_mp, rows, half), bf16),
             dma((3,)),
             dma((chunks, 2)),
-            dma,
-            dma,
+            dma((n_mp,)),
+            dma((n_mp,)),
             dma((chunks, 2, max(n_grp, w_seq))),
             dma((chunks, 2, max(n_grp, w_seq))),
             dma((chunks, 2, max(n_grp, w_seq))),

time: 108 us -> 84.5 us (0.78)
  the two profiles are of different devices: /device:TPU:5 before, /device:TPU:27 now
where the time goes in v2:
time: 84.5 us; the launch traced here: 84.2 us
  Pallas kernels  78 us (92%)
  local copies, waits for them, and re-layouts  4.95 us (6%)
  between operations  1.29 us (2%)
    pallas_call x1, Pallas kernels, on_device(): pl.pallas_call(functools.partial(kernel, (n_grp, n_seq, n_mp, w_seq, chun...  78 us
    unnamed x2, local copies, waits for them, and re-layouts  4.95 us

profile of v2, /device:TPU:27, one launch (start us, length us, event | category | flops | bytes accessed | tf_op | source)
XLA Modules:
  0.0 84.2 jit_solution(2422407525021547754)
XLA Ops:
  1.3 78.0 %shard_map.95 = (bf16[256,1024]{1,0:T(8,128)(2,1)}, f32[4,256,512]{2,1,0:T(8,128)}) custom-call(f32[8]{0:T(128)} %lambdas.1, s32[1]{0:T(128)S(6)} %copy.12.counts, bf16[256,1024]{1,0:T(8,128)(2,1)} %bitcast.8, bf16[4,256,1024]{2,1,0:T(8,128)(2,1)} %bitcast.6, bf16[64,1024]{1,0:T(8,128)(2,1)} %wk_hbm.1, bf16[64,1024]{1,0:T(8,128)(2,1)} %wv_hbm.1, ...), custom_call_target="tpu_custom_call" | custom-call | tf_op jit(solution)/shard_map/pallas_call | solution.py:321
  79.3 1.9 %copy.13 = bf16[1,256,1024]{2,1,0:T(8,128)(2,1)} copy(bf16[1,256,1024]{2,1,0:T(8,128)(2,1)} %bitcast.10) | data formatting | bytes 1048576
  81.2 3.1 %copy.14 = f32[1,4,256,512]{3,2,1,0:T(8,128)} copy(f32[1,4,256,512]{3,2,1,0:T(8,128)} %bitcast.7) | data formatting | bytes 4194304
